TPU v7x, 32 devices: a whole 2x2x4 slice. The times are simulated.
32 devices in a mesh: group: 2 (over x), tile: 16 (over z, y, core).
Axes of the slice: x: 2, y: 2, z: 4, core: 2. Of those that a mesh axis runs over, the one named last changes fastest.
Arguments:
- hadamard: int32 [128, 1152], P(None, 'tile'), may hold values from -1 to 1, as said below
- stroke: float32 [2304], P(('group', 'tile')), parts along dimension 0, may hold values from 0.3 to 1
- influence: bfloat16 [3, 2304, 8192], P(None, ('group', 'tile')), parts along dimension 1, may hold values from -0.4375 to 0.4375
- amplitude: float32 [1024, 16, 16], P(('group', 'tile')), parts along dimension 0, may hold values from 0.3 to 1
- aberration: float32 [1024, 16, 16], P(('group', 'tile')), parts along dimension 0, may hold values from -3 to 3
- valid_mask: int32 [1024], P(('group', 'tile')), parts along dimension 0, may hold values from 0 to 1, as said below
Outputs:
- imat: float32 [2304, 2, 512], P(('group', 'tile')), parts along dimension 0
There are 2 independent parts, one for each index of `group`. A program takes and returns all parts, laid end to end along the dimension named above; an argument that names none is the same for every part. Nothing has to cross between parts.
Inputs may be any that keep to these rules, and one draw needn't show every extreme that they name: `hadamard`: each column is one column of a Sylvester-Hadamard matrix whose order is the least power of two not below 1152, restricted to 128 distinct rows of it; different actuators take different columns. `valid_mask`: every pupil tile of 32 subapertures holds at least one valid subaperture.
All inputs are finite; a program needn't handle non-finite values.
Results may differ from a plain program's by a relative error of at most 0.0055.
Values may be sent and summed in bfloat16 or wider, within the bound.
A program may use at most 128 MiB of HBM per device.

v0:
```python
import math

import jax
import jax.numpy as jnp
from jax import lax
from jax.sharding import PartitionSpec as P

PIX = 16


HIGHEST = lax.Precision.HIGHEST


def passed_along(value, axis, steps):
    count = lax.axis_size(axis)
    first, last = (max(0, -steps), min(count, count - steps))
    return lax.ppermute(value, axis, [(source, source + steps) for source in range(first, last)])


def shortened(x):
    return jax.tree.map(lambda a: a.astype(jnp.bfloat16) if a.dtype == jnp.float32 else a, x)


def transform_tables(samples, pixels):
    freqs = jnp.arange(pixels, dtype=jnp.float32) - pixels / 2.0
    places = jnp.arange(samples, dtype=jnp.float32)
    angle = 2.0 * jnp.pi * freqs[:, None] * places[None, :] / (2.0 * samples)
    return (jnp.cos(angle), -jnp.sin(angle))


def kron_tables(samples, pixels):
    table_real, table_imag = transform_tables(samples, pixels)
    kron_real = jnp.kron(table_real, table_real) - jnp.kron(table_imag, table_imag)
    kron_imag = jnp.kron(table_real, table_imag) + jnp.kron(table_imag, table_real)
    upper = jnp.concatenate([kron_real.T, kron_imag.T], axis=1)
    lower = jnp.concatenate([-kron_imag.T, kron_real.T], axis=1)
    transform = jnp.concatenate([upper, lower], axis=0)
    centre = jnp.arange(pixels, dtype=jnp.float32) - (pixels - 1) / 2.0
    along_u = jnp.repeat(centre, pixels)
    along_v = jnp.tile(centre, pixels)
    moments = jnp.stack([jnp.ones_like(along_u), along_u, along_v], axis=1)
    return (transform, moments)


def spot_slopes(phase_map, amplitude, aberration, valid_mask):
    patterns, sub_count, samples = (phase_map.shape[0], phase_map.shape[1], phase_map.shape[2])
    flat = samples * samples
    transform, moments = kron_tables(samples, PIX)
    half = PIX * PIX
    phase_rows = phase_map.reshape(patterns, sub_count, flat)
    amp_rows = amplitude.reshape(sub_count, flat)[None]
    abe_rows = aberration.reshape(sub_count, flat)[None]
    results = []
    for pattern_sign in (1.0, -1.0):
        angles = abe_rows + pattern_sign * phase_rows
        field = jnp.concatenate([amp_rows * jnp.cos(angles), amp_rows * jnp.sin(angles)], axis=2)
        focal = jnp.dot(field.reshape(patterns * sub_count, 2 * flat), transform, precision=HIGHEST)
        intensity = focal[:, :half] * focal[:, :half] + focal[:, half:] * focal[:, half:]
        sums = jnp.dot(intensity, moments, precision=HIGHEST)
        centroid_x = sums[:, 1] / sums[:, 0]
        centroid_y = sums[:, 2] / sums[:, 0]
        results.append(
            jnp.stack([centroid_x, centroid_y], axis=1)
            .reshape(patterns, sub_count, 2)
            .transpose(0, 2, 1)
        )
    weights = valid_mask.astype(jnp.float32)[None, None, :]
    return ((results[0] - results[1]) * 0.5 * weights).astype(jnp.bfloat16)


def shape_term(commands, slab):
    term = jnp.dot(commands, slab, preferred_element_type=jnp.float32).astype(jnp.bfloat16)
    return lax.optimization_barrier(term)


def per_device(hadamard, stroke, influence, amplitude, aberration, valid_mask):
    patterns = hadamard.shape[0]
    sub_count = amplitude.shape[0]
    samples = amplitude.shape[1]
    commands = (stroke[None, :] * hadamard.astype(jnp.float32)).astype(jnp.bfloat16)
    local_term = shape_term(commands, influence[1])
    lower_cmds, lower_slab = passed_along((commands, influence[2]), "tile", 1)
    upper_cmds, upper_slab = passed_along((commands, influence[0]), "tile", -1)
    from_lower = shape_term(lower_cmds, lower_slab)
    from_upper = shape_term(upper_cmds, upper_slab)
    phase_map = (
        local_term.astype(jnp.float32)
        + from_lower.astype(jnp.float32)
        + from_upper.astype(jnp.float32)
    )
    block_rows = math.gcd(patterns, 64)
    blocks = phase_map.reshape(patterns // block_rows, block_rows, sub_count, samples, samples)

    def one_block(pattern_block):
        return spot_slopes(pattern_block, amplitude, aberration, valid_mask)

    slopes = lax.map(one_block, blocks).reshape(patterns, 2, sub_count)
    signs_half = hadamard.astype(jnp.bfloat16)
    summed = jnp.einsum(
        "pa,pcs->acs",
        signs_half,
        lax.all_gather(shortened(slopes), "tile", axis=2, tiled=True),
        preferred_element_type=jnp.float32,
    )
    return summed / (patterns * stroke)[:, None, None]


def solution(mesh):
    placed = (
        P(None, "tile"),
        P(("group", "tile")),
        P(None, ("group", "tile"), None),
        P(("group", "tile"), None, None),
        P(("group", "tile"), None, None),
        P(("group", "tile")),
    )
    return jax.shard_map(
        per_device,
        mesh=mesh,
        in_specs=placed,
        out_specs=P(("group", "tile"), None, None),
        check_vma=False,
    )
```

profile of v0, /device:TPU:0, one launch (start us, length us, event | category | flops | bytes accessed | tf_op | source)
XLA Modules:
  0.0 236.9 jit_solution(5249718799039673560)
XLA Ops:
  0.0 2.8 %slice_bitcast_fusion.1 = (bf16[72,8192]{1,0:T(8,128)(2,1)}, bf16[72,8192]{1,0:T(8,128)(2,1)S(1)}) fusion(bf16[3,72,8192]{2,1,0:T(8,128)(2,1)} %param.10), kind=kLoop, calls=%fused_computation.58 | loop fusion | bytes 4718592 | tf_op jit(solution)/shard_map/squeeze | solution.py:82
  2.8 3.6 %collective-permute-start.1 = (bf16[72,8192]{1,0:T(8,128)(2,1)}, bf16[72,8192]{1,0:T(8,128)(2,1)}, u32[]{:S(2)}, u32[]{:S(2)}) collective-permute-start(bf16[72,8192]{1,0:T(8,128)(2,1)} %get-tuple-element.136), channel_id=1, source_target_pairs={{0,1},{1,2},{2,3},{3,4},{4,5},{5,6},{6,7},{7,8},{8,9},{9,10},{10,1... | collective-permute-start | bytes 3538952 | tf_op jit(solution)/shard_map/ppermute | solution.py:17
  6.4 1.3 collective-permute-start.3
  7.7 0.1 multiply_convert_fusion
  7.8 4.1 %collective-permute-start = (bf16[128,72]{0,1:T(8,128)(2,1)S(1)}, bf16[128,72]{0,1:T(8,128)(2,1)S(1)}, u32[]{:S(2)}, u32[]{:S(2)}) collective-permute-start(bf16[128,72]{0,1:T(8,128)(2,1)S(1)} %multiply_convert_fusion), channel_id=1, source_target_pairs={{0,1},{1,2},{2,3},{3,4},{4,5},{5,6},{6,7},{7,8},{8,9},{9,10},{10,1... | collective-permute-start | bytes 55304 | tf_op jit(solution)/shard_map/ppermute | solution.py:17
  11.9 1.3 collective-permute-start.2
  13.2 2.0 convolution_convert_fusion.2
  15.3 2.0 convolution_convert_fusion.1
  17.3 2.0 convolution_convert_fusion
  19.3 2.8 %convert_add_fusion = f32[128,8192]{1,0:T(8,128)} fusion(bf16[128,8192]{1,0:T(8,128)(2,1)S(1)} %convolution_convert_fusion, bf16[128,8192]{1,0:T(8,128)(2,1)S(1)} %convolution_convert_fusion.1, bf16[128,8192]{1,0:T(8,128)(2,1)S(1)} %convolution_convert_fusion.2), kind=kLoop, calls=%fused_computation.55 | loop fusion | flops 5242880 | bytes 10485760 | tf_op jit(solution)/shard_map/add | solution.py:87
  22.1 5.6 %copy.28 = f32[128,8192]{0,1:T(8,128)} copy(f32[128,8192]{1,0:T(8,128)} %convert_add_fusion) | data formatting | bytes 8388608 | tf_op jit(solution)/shard_map/add | solution.py:87
  27.7 9.2 %reshape.211 = f32[2,64,32,16,16]{1,0,4,3,2:T(2,128)} reshape(f32[128,8192]{0,1:T(8,128)} %copy.28) | data formatting | bytes 8388608 | tf_op jit(solution)/shard_map/reshape | solution.py:92
  36.9 159.1 %while.12 = (s32[]{:T(128)}, bf16[2,64,2,32]{1,0,3,2:T(2,128)(2,1)S(1)}, f32[32,16,16]{0,2,1:T(8,128)S(1)}, f32[32,16,16]{0,2,1:T(8,128)S(1)}, f32[2,64,32,16,16...) while((s32[]{:T(128)}, ...), condition=%wide.region_1.2_spmd, body=%wide.region_0.1_spmd.sunk | while | flops 12933627904 | bytes 64969588 | solution.py:97
  36.9 9.7 %constant_dynamic-slice_fusion.2 = f32[1,64,32,16,16]{1,0,4,3,2:T(1,128)} fusion(f32[2,64,32,16,16]{1,0,4,3,2:T(2,128)} %get-tuple-element.223, s32[]{:T(128)} %get-tuple-element.209), kind=kLoop, calls=%fused_computation.46.clone.1 | loop fusion | bytes 4194308 | tf_op jit(solution)/shard_map/while/body/jit(dynamic_index_in_dim)/dynamic_slice | solution.py:97
  46.6 12.3 %copy.40 = f32[1,64,32,16,16]{2,1,4,3,0:T(8,128)} copy(f32[1,64,32,16,16]{1,0,4,3,2:T(1,128)} %constant_dynamic-slice_fusion.2) | data formatting | bytes 4194304 | tf_op jit(solution)/shard_map/while/body/jit(dynamic_index_in_dim)/dynamic_slice | solution.py:97
  58.9 7.5 %reshape.239 = f32[2048,256]{0,1:T(8,128)} reshape(f32[1,64,32,16,16]{2,1,4,3,0:T(8,128)} %copy.40) | data formatting | bytes 4194304 | tf_op jit(solution)/shard_map/while/body/eval_jaxpr/reshape | solution.py:50
  66.4 1.9 copy.41
  68.4 0.1 copy.43
  68.5 16.6 %bitcast_multiply_fusion.5 = (f32[2048,256]{1,0:T(8,128)}, f32[2048,256]{1,0:T(8,128)}, f32[2048,256]{1,0:T(8,128)}, f32[2048,256]{1,0:T(8,128)}) fusion(f32[2048,256]{1,0:T(8,128)S(1)} %copy.41, f32[32,256]{1,0:T(8,128)S(1)} %copy.42, f32[32,256]{1,0:T(8,128)S(1)} %copy.43), kind=kLoop, calls=%fused_computation.3.clone.1 | loop fusion | flops 3670016 | bytes 10551296 | tf_op jit(solution)/shard_map/while/body/eval_jaxpr/mul | solution.py:56
  85.1 0.1 fusion.54
  85.3 2.0 multiply_add_fusion.2
  87.2 2.4 %add.133 = f32[256,256]{1,0:T(8,128)S(1)} reshape(f32[16,16,16,16]{3,2,1,0:T(8,128)} %get-tuple-element.192) | data formatting | bytes 524288 | tf_op jit(solution)/shard_map/while/body/eval_jaxpr/add | solution.py:34
  89.7 0.9 sub.43
  90.7 9.8 %fusion.57 = f32[2048,512]{1,0:T(8,128)} fusion(f32[2048,256]{1,0:T(8,128)} %get-tuple-element.193, f32[2048,256]{1,0:T(8,128)} %get-tuple-element.194, f32[256,256]{0,1:T(8,128)S(1)} %bitcast.82, f32[256,256]{0,1:T(8,128)S(1)} %bitcast_negate_fusion.2, f32[256,256]{0,1:T(8,128)S(1)} %bitcast.80), kind=kOutput, calls=%fused_computation.8.clone.1 | convolution fusion | flops 6444285952 | bytes 9175040 | tf_op jit(solution)/shard_map/while/body/eval_jaxpr/dot_general | solution.py:57
  100.5 0.1 broadcast_in_dim.33
  100.5 0.1 reshape.240
  100.6 0.1 tile.19
  100.7 4.4 %fusion.58 = f32[2048,3]{0,1:T(4,128)S(1)} fusion(f32[2048,512]{1,0:T(8,128)} %fusion.57, f32[256,1]{0,1:T(1,128)S(1)} %tile.19, f32[256,1]{0,1:T(1,128)S(1)} %reshape.240, f32[3]{0:T(128)S(1)} %pad.6.clone.2), kind=kOutput, calls=%fused_computation.16.clone.1 | convolution fusion | flops 20448768 | bytes 4220940 | tf_op jit(solution)/shard_map/while/body/eval_jaxpr/dot_general | solution.py:59
  105.1 8.5 %fusion.55 = f32[2048,512]{1,0:T(8,128)S(1)} fusion(f32[2048,256]{1,0:T(8,128)} %get-tuple-element.187, f32[2048,256]{1,0:T(8,128)S(1)} %copy-done, f32[256,256]{0,1:T(8,128)S(1)} %bitcast.83, f32[256,256]{0,1:T(8,128)S(1)} %bitcast_negate_fusion.2, f32[256,256]{0,1:T(8,128)S(1)} %bitcast.81), kind=kOutput, calls=%fused_computation.4.clone.1 | convolution fusion | flops 6444285952 | bytes 9175040 | tf_op jit(solution)/shard_map/while/body/eval_jaxpr/dot_general | solution.py:57
  113.6 2.0 fusion.56
  115.7 0.1 fusion.59
  115.8 0.1 stack.28
  115.8 0.1 stack.29
  115.9 0.1 stack.30
  116.0 0.1 stack.31
  116.1 0.1 copy.44
  116.2 0.2 dynamic_update_slice.8
  116.5 9.7 %constant_dynamic-slice_fusion.2 = f32[1,64,32,16,16]{1,0,4,3,2:T(1,128)} fusion(f32[2,64,32,16,16]{1,0,4,3,2:T(2,128)} %get-tuple-element.223, s32[]{:T(128)} %get-tuple-element.209), kind=kLoop, calls=%fused_computation.46.clone.1 | loop fusion | bytes 4194308 | tf_op jit(solution)/shard_map/while/body/jit(dynamic_index_in_dim)/dynamic_slice | solution.py:97
  126.2 12.3 %copy.40 = f32[1,64,32,16,16]{2,1,4,3,0:T(8,128)} copy(f32[1,64,32,16,16]{1,0,4,3,2:T(1,128)} %constant_dynamic-slice_fusion.2) | data formatting | bytes 4194304 | tf_op jit(solution)/shard_map/while/body/jit(dynamic_index_in_dim)/dynamic_slice | solution.py:97
  138.5 7.5 %reshape.239 = f32[2048,256]{0,1:T(8,128)} reshape(f32[1,64,32,16,16]{2,1,4,3,0:T(8,128)} %copy.40) | data formatting | bytes 4194304 | tf_op jit(solution)/shard_map/while/body/eval_jaxpr/reshape | solution.py:50
  146.0 1.9 copy.41
  148.0 0.1 copy.43
  148.1 16.6 %bitcast_multiply_fusion.5 = (f32[2048,256]{1,0:T(8,128)}, f32[2048,256]{1,0:T(8,128)}, f32[2048,256]{1,0:T(8,128)}, f32[2048,256]{1,0:T(8,128)}) fusion(f32[2048,256]{1,0:T(8,128)S(1)} %copy.41, f32[32,256]{1,0:T(8,128)S(1)} %copy.42, f32[32,256]{1,0:T(8,128)S(1)} %copy.43), kind=kLoop, calls=%fused_computation.3.clone.1 | loop fusion | flops 3670016 | bytes 10551296 | tf_op jit(solution)/shard_map/while/body/eval_jaxpr/mul | solution.py:56
  164.7 0.1 fusion.54
  164.8 2.0 multiply_add_fusion.2
  166.8 2.4 %add.133 = f32[256,256]{1,0:T(8,128)S(1)} reshape(f32[16,16,16,16]{3,2,1,0:T(8,128)} %get-tuple-element.192) | data formatting | bytes 524288 | tf_op jit(solution)/shard_map/while/body/eval_jaxpr/add | solution.py:34
  169.3 0.9 sub.43
  170.2 9.8 %fusion.57 = f32[2048,512]{1,0:T(8,128)} fusion(f32[2048,256]{1,0:T(8,128)} %get-tuple-element.193, f32[2048,256]{1,0:T(8,128)} %get-tuple-element.194, f32[256,256]{0,1:T(8,128)S(1)} %bitcast.82, f32[256,256]{0,1:T(8,128)S(1)} %bitcast_negate_fusion.2, f32[256,256]{0,1:T(8,128)S(1)} %bitcast.80), kind=kOutput, calls=%fused_computation.8.clone.1 | convolution fusion | flops 6444285952 | bytes 9175040 | tf_op jit(solution)/shard_map/while/body/eval_jaxpr/dot_general | solution.py:57
  180.0 0.1 broadcast_in_dim.33
  180.1 0.1 reshape.240
  180.2 0.1 tile.19
  180.3 4.4 %fusion.58 = f32[2048,3]{0,1:T(4,128)S(1)} fusion(f32[2048,512]{1,0:T(8,128)} %fusion.57, f32[256,1]{0,1:T(1,128)S(1)} %tile.19, f32[256,1]{0,1:T(1,128)S(1)} %reshape.240, f32[3]{0:T(128)S(1)} %pad.6.clone.2), kind=kOutput, calls=%fused_computation.16.clone.1 | convolution fusion | flops 20448768 | bytes 4220940 | tf_op jit(solution)/shard_map/while/body/eval_jaxpr/dot_general | solution.py:59
  184.7 8.5 %fusion.55 = f32[2048,512]{1,0:T(8,128)S(1)} fusion(f32[2048,256]{1,0:T(8,128)} %get-tuple-element.187, f32[2048,256]{1,0:T(8,128)S(1)} %copy-done, f32[256,256]{0,1:T(8,128)S(1)} %bitcast.83, f32[256,256]{0,1:T(8,128)S(1)} %bitcast_negate_fusion.2, f32[256,256]{0,1:T(8,128)S(1)} %bitcast.81), kind=kOutput, calls=%fused_computation.4.clone.1 | convolution fusion | flops 6444285952 | bytes 9175040 | tf_op jit(solution)/shard_map/while/body/eval_jaxpr/dot_general | solution.py:57
  193.2 2.0 fusion.56
  195.2 0.1 fusion.59
  195.3 0.1 stack.28
  195.4 0.1 stack.29
  195.6 0.1 stack.31
  195.7 0.1 copy.44
  195.8 0.2 dynamic_update_slice.8
  196.0 0.1 reshape.212
  196.1 39.6 %all_gather.3 = bf16[128,2,512]{0,2,1:T(8,128)(2,1)S(1)} all-gather(bf16[128,2,32]{0,2,1:T(8,128)(2,1)S(1)} %reshape.212), channel_id=1, replica_groups=mesh['group'=2,'tile'=16] {'tile'}, dimensions={2}, use_global_device_ids=true | all-gather | bytes 278528 | tf_op jit(solution)/shard_map/all_gather | solution.py:102
  235.7 0.3 fusion.30
  236.0 0.9 copy.31
  (38 shorter events, 0.4 us)
Async XLA Ops:
  0.0 7.7 %copy-start.3 = (s32[128,72]{0,1:T(8,128)S(1)}, s32[128,72]{0,1:T(8,128)}, u32[]{:S(2)}) copy-start(s32[128,72]{0,1:T(8,128)} %param.8) | copy-start | bytes 110596
  0.0 7.7 %copy-start.4 = (f32[72]{0:T(128)S(1)}, f32[72]{0:T(128)}, u32[]{:S(2)}) copy-start(f32[72]{0:T(128)} %param.9) | copy-start | bytes 868
  2.8 12.4 %copy-start.5 = (s32[32]{0:T(128)S(1)}, s32[32]{0:T(128)}, u32[]{:S(2)}) copy-start(s32[32]{0:T(128)} %param.13) | copy-start | bytes 388
  2.8 12.4 %collective-permute-start.1 = (bf16[72,8192]{1,0:T(8,128)(2,1)}, bf16[72,8192]{1,0:T(8,128)(2,1)}, u32[]{:S(2)}, u32[]{:S(2)}) collective-permute-start(bf16[72,8192]{1,0:T(8,128)(2,1)} %get-tuple-element.136), channel_id=1, source_target_pairs={{0,1},{1,2},{2,3},{3,4},{4,5},{5,6},{6,7},{7,8},{8,9},{9,10},{10,1... | collective-permute-start | bytes 3538952 | tf_op jit(solution)/shard_map/ppermute | solution.py:17
  6.4 10.9 %collective-permute-start.3 = (bf16[72,8192]{1,0:T(8,128)(2,1)S(1)}, bf16[72,8192]{1,0:T(8,128)(2,1)}, u32[]{:S(2)}, u32[]{:S(2)}) collective-permute-start(bf16[72,8192]{1,0:T(8,128)(2,1)S(1)} %get-tuple-element.137), channel_id=1, source_target_pairs={{1,0},{2,1},{3,2},{4,3},{5,4},{6,5},{7,6},{8,7},{9,8},{10,9},{11,1... | collective-permute-start | bytes 3538952 | tf_op jit(solution)/shard_map/ppermute | solution.py:17
  7.8 7.5 %collective-permute-start = (bf16[128,72]{0,1:T(8,128)(2,1)S(1)}, bf16[128,72]{0,1:T(8,128)(2,1)S(1)}, u32[]{:S(2)}, u32[]{:S(2)}) collective-permute-start(bf16[128,72]{0,1:T(8,128)(2,1)S(1)} %multiply_convert_fusion), channel_id=1, source_target_pairs={{0,1},{1,2},{2,3},{3,4},{4,5},{5,6},{6,7},{7,8},{8,9},{9,10},{10,1... | collective-permute-start | bytes 55304 | tf_op jit(solution)/shard_map/ppermute | solution.py:17
  11.9 5.4 %collective-permute-start.2 = (bf16[128,72]{0,1:T(8,128)(2,1)S(1)}, bf16[128,72]{0,1:T(8,128)(2,1)S(1)}, u32[]{:S(2)}, u32[]{:S(2)}) collective-permute-start(bf16[128,72]{0,1:T(8,128)(2,1)S(1)} %multiply_convert_fusion), channel_id=1, source_target_pairs={{1,0},{2,1},{3,2},{4,3},{5,4},{6,5},{7,6},{8,7},{9,8},{10,9},{11,1... | collective-permute-start | bytes 55304 | tf_op jit(solution)/shard_map/ppermute | solution.py:17
  27.7 9.2 %copy-start.1 = (f32[32,16,16]{0,2,1:T(8,128)S(1)}, f32[32,16,16]{0,2,1:T(8,128)}, u32[]{:S(2)}) copy-start(f32[32,16,16]{0,2,1:T(8,128)} %param.11) | copy-start | bytes 98308
  27.7 9.2 %copy-start.2 = (f32[32,16,16]{0,2,1:T(8,128)S(1)}, f32[32,16,16]{0,2,1:T(8,128)}, u32[]{:S(2)}) copy-start(f32[32,16,16]{0,2,1:T(8,128)} %param.12) | copy-start | bytes 98308
  100.5 4.7 %copy-start = (f32[2048,256]{1,0:T(8,128)S(1)}, f32[2048,256]{1,0:T(8,128)}, u32[]{:S(2)}) copy-start(f32[2048,256]{1,0:T(8,128)} %get-tuple-element.188) | copy-start | bytes 6291460 | tf_op jit(solution)/shard_map/while
  180.0 4.7 %copy-start = (f32[2048,256]{1,0:T(8,128)S(1)}, f32[2048,256]{1,0:T(8,128)}, u32[]{:S(2)}) copy-start(f32[2048,256]{1,0:T(8,128)} %get-tuple-element.188) | copy-start | bytes 6291460 | tf_op jit(solution)/shard_map/while
where the time goes:
time: 238 us; the launch traced here: 237 us
  local copies, waits for them, and re-layouts  90.3 us (38%)
  matrix products  55.7 us (23%)
  other arithmetic  40.7 us (17%)
  blocking collectives  39.6 us (17%)
  starting transfers between devices  10.3 us (4%)
    dynamic_slice x4, local copies, waits for them, and re-layouts, per_device(): slopes = lax.map(one_block, blocks).reshape(patterns, 2, sub_count)  44.1 us
    all_gather x1, blocking collectives, per_device(): lax.all_gather(shortened(slopes), 'tile', axis=2, tiled=True)  39.6 us
    dot_general x4, matrix products, spot_slopes(): jnp.dot(field.reshape(patterns * sub_count, 2 * flat), transform, precisi...  36.6 us
    mul x2, other arithmetic, spot_slopes(): amp_rows * jnp.cos(angles)  33.3 us
    reshape x4, local copies, waits for them, and re-layouts, spot_slopes(): phase_rows = phase_map.reshape(patterns, sub_count, flat)  18.8 us
    dot_general x4, matrix products, spot_slopes(): sums = jnp.dot(intensity, moments, precision=HIGHEST)  12.9 us
    ppermute x4, starting transfers between devices, passed_along(): lax.ppermute(value, axis, [(source, source + steps) for source in range(f...  10.3 us
    reshape x1, local copies, waits for them, and re-layouts, per_device(): phase_map.reshape(patterns // block_rows, block_rows, sub_count, samples,...  9.2 us
  transfers between devices with their start and end apart: 4, of which 0 were waited for; matrix products, arithmetic and copies ran while one was open for 2% of the time, Pallas kernels for 0%

commit v1 on v0

v1 whole, which is shorter than its diff:
```python
import functools
import math

import jax
import jax.numpy as jnp
import numpy as np
from jax import lax
from jax.experimental import pallas as pl
from jax.experimental.pallas import tpu as pltpu
from jax.sharding import PartitionSpec as P

PIX = 16
MESH = pl.DeviceIdType.MESH
NT = (((1,), (1,)), ((), ()))


def dft_table(samples, pixels):
    freqs = np.arange(pixels) - pixels / 2.0
    wave = np.exp(-2j * np.pi * freqs[:, None] * np.arange(samples)[None, :] / (2.0 * samples))
    kron = np.kron(wave, wave)
    return np.block([[kron.real, -kron.imag], [kron.imag, kron.real]]).astype(np.float32)


def poly_fit(func, degree):
    fit = np.polynomial.chebyshev.Chebyshev.interpolate(func, degree, domain=[0.0, 0.25])
    return [float(c) for c in fit.convert(kind=np.polynomial.Polynomial).coef]


def sin_over_r(z):
    return 2 * np.pi * np.sinc(2 * np.sqrt(z))


COS = poly_fit(lambda z: np.cos(2 * np.pi * np.sqrt(z)), 5)
SIN = poly_fit(sin_over_r, 5)


def horner(coefs, z):
    total = coefs[-1] * z + coefs[-2]
    for c in coefs[-3::-1]:
        total = total * z + c
    return total


def cos_sin(phase):
    turns = phase * (1.0 / (2.0 * math.pi))
    r = turns - jnp.round(turns)
    z = r * r
    return horner(COS, z), r * horner(SIN, z)


def column_sums(planes):
    pix = len(planes)
    run = planes[-1]
    nested = run
    for plane in planes[-2::-1]:
        run = run + plane
        nested = nested + run
    places = lax.broadcasted_iota(jnp.int32, run.shape, 0).astype(jnp.float32)
    centre = (pix - 1) / 2.0
    along_u = nested - (centre + 1.0) * run
    along_v = run * (places - centre)
    return [jnp.sum(x, axis=0, keepdims=True) for x in (run, along_u, along_v)]


def spot_rows(phase, real, imag, table):
    patterns = phase.shape[0]
    cs, sn = cos_sin(phase)
    even = jnp.concatenate([(cs * real).astype(jnp.bfloat16), (cs * imag).astype(jnp.bfloat16)], axis=1)
    odd = jnp.concatenate([(sn * -imag).astype(jnp.bfloat16), (sn * real).astype(jnp.bfloat16)], axis=1)
    field = jnp.concatenate([even, odd], axis=0)
    focal = lax.dot_general(table, field, NT, preferred_element_type=jnp.float32)
    half = focal.shape[0] // 2
    squares, crosses = [], []
    for u in range(PIX):
        re = focal[u * PIX:(u + 1) * PIX]
        im = focal[half + u * PIX:half + (u + 1) * PIX]
        c_re, s_re = re[:, :patterns], re[:, patterns:]
        c_im, s_im = im[:, :patterns], im[:, patterns:]
        squares.append((c_re * c_re + c_im * c_im) + (s_re * s_re + s_im * s_im))
        crosses.append(c_re * s_re + c_im * s_im)
    p0, pu, pv = column_sums(squares)
    q0, qu, qv = [2.0 * x for x in column_sums(crosses)]
    scale = 1.0 / ((p0 + q0) * (p0 - q0))
    return (qu * p0 - pu * q0) * scale, (qv * p0 - pv * q0) * scale


def slopes_kernel(per_step, flat, cmd_ref, mid_ref, low_ref, up_ref, real_ref, imag_ref, mask_ref, table_ref, out_ref):
    rows_u, rows_v = [], []
    for k in range(per_step):
        cols = pl.ds(k * flat, flat)
        phase = jnp.dot(cmd_ref[0], low_ref[:, cols], preferred_element_type=jnp.float32)
        phase += jnp.dot(cmd_ref[1], mid_ref[0, :, cols], preferred_element_type=jnp.float32)
        phase += jnp.dot(cmd_ref[2], up_ref[:, cols], preferred_element_type=jnp.float32)
        along_u, along_v = spot_rows(phase, real_ref[k:k + 1, :], imag_ref[k:k + 1, :], table_ref[...])
        rows_u.append(along_u)
        rows_v.append(along_v)
    mask = mask_ref[...]
    out_ref[0] = (jnp.concatenate(rows_u, axis=0) * mask).astype(out_ref.dtype)
    out_ref[1] = (jnp.concatenate(rows_v, axis=0) * mask).astype(out_ref.dtype)


def gather_kernel(n, mine_ref, had_ref, out_ref, held, own_sem, send_sems, recv_sems):
    me = lax.axis_index("tile")
    subs = mine_ref.shape[1]
    barrier = pltpu.get_barrier_semaphore()

    @pl.loop(1, n)
    def _(k):
        pl.semaphore_signal(barrier, inc=1, device_id={"tile": lax.rem(me + k, n)}, device_id_type=MESH)

    pl.semaphore_wait(barrier, n - 1)
    slot = held.at[:, pl.ds(pl.multiple_of(me * subs, subs), subs), :]
    own = pltpu.make_async_copy(mine_ref, slot, own_sem)
    own.start()

    def push(k):
        return pltpu.make_async_remote_copy(
            src_ref=mine_ref,
            dst_ref=slot,
            send_sem=send_sems.at[k],
            recv_sem=recv_sems.at[k],
            device_id={"tile": lax.rem(me + k, n)},
            device_id_type=MESH,
        )

    @pl.loop(1, n)
    def _(k):
        push(k).start()

    own.wait()

    @pl.loop(1, n)
    def _(k):
        push(k).wait()

    for c in range(2):
        out_ref[c] = lax.dot_general(had_ref[...], held[c], NT, preferred_element_type=jnp.float32)


def passed_along(value, axis, steps):
    count = lax.axis_size(axis)
    first, last = (max(0, -steps), min(count, count - steps))
    return lax.ppermute(value, axis, [(source, source + steps) for source in range(first, last)])


def per_device(hadamard, stroke, influence, amplitude, aberration, valid_mask):
    n = lax.axis_size("tile")
    patterns, acts = hadamard.shape
    subs, samples = amplitude.shape[0], amplitude.shape[1]
    flat = samples * samples
    per_step = math.gcd(subs, 16)
    commands = (stroke[None, :] * hadamard.astype(jnp.float32)).astype(jnp.bfloat16)
    low_slab, up_slab = passed_along(influence[2], "tile", 1), passed_along(influence[0], "tile", -1)
    low_cmds, up_cmds = passed_along(commands, "tile", 1), passed_along(commands, "tile", -1)
    cmds = jnp.stack([low_cmds, commands, up_cmds])
    amp, abe = amplitude.reshape(subs, flat), aberration.reshape(subs, flat)
    real, imag = amp * jnp.cos(abe), amp * jnp.sin(abe)
    mask = valid_mask.astype(jnp.float32)[:, None]
    table = jnp.asarray(dft_table(samples, PIX), dtype=jnp.bfloat16)
    width = per_step * flat
    slopes = pl.pallas_call(
        functools.partial(slopes_kernel, per_step, flat),
        grid=(subs // per_step,),
        out_shape=jax.ShapeDtypeStruct((2, subs, patterns), jnp.bfloat16),
        in_specs=[
            pl.BlockSpec((3, patterns, acts), lambda i: (0, 0, 0)),
            pl.BlockSpec((1, acts, width), lambda i: (1, 0, i)),
            pl.BlockSpec((acts, width), lambda i: (0, i)),
            pl.BlockSpec((acts, width), lambda i: (0, i)),
            pl.BlockSpec((per_step, flat), lambda i: (i, 0)),
            pl.BlockSpec((per_step, flat), lambda i: (i, 0)),
            pl.BlockSpec((per_step, 1), lambda i: (i, 0)),
            pl.BlockSpec((2 * flat, 2 * flat), lambda i: (0, 0)),
        ],
        out_specs=pl.BlockSpec((2, per_step, patterns), lambda i: (0, i, 0)),
        compiler_params=pltpu.CompilerParams(vmem_limit_bytes=40 * 1024 * 1024),
        name="slopes",
    )(cmds, influence, low_slab, up_slab, real, imag, mask, table)
    signs = hadamard.T.astype(jnp.bfloat16)
    summed = pl.pallas_call(
        functools.partial(gather_kernel, n),
        out_shape=jax.ShapeDtypeStruct((2, acts, n * subs), jnp.float32),
        in_specs=[pl.BlockSpec(memory_space=pltpu.VMEM)] * 2,
        out_specs=pl.BlockSpec(memory_space=pltpu.VMEM),
        scratch_shapes=[
            pltpu.VMEM((2, n * subs, patterns), jnp.bfloat16),
            pltpu.SemaphoreType.DMA,
            pltpu.SemaphoreType.DMA((n,)),
            pltpu.SemaphoreType.DMA((n,)),
        ],
        compiler_params=pltpu.CompilerParams(collective_id=0, has_side_effects=True),
        name="gather",
    )(slopes, signs)
    return summed.transpose(1, 0, 2) / (patterns * stroke)[:, None, None]


def solution(mesh):
    placed = (
        P(None, "tile"),
        P(("group", "tile")),
        P(None, ("group", "tile"), None),
        P(("group", "tile"), None, None),
        P(("group", "tile"), None, None),
        P(("group", "tile")),
    )
    return jax.shard_map(
        per_device,
        mesh=mesh,
        in_specs=placed,
        out_specs=P(("group", "tile"), None, None),
        check_vma=False,
    )
```

time: 238 us -> 73.7 us (0.31)
  local copies, waits for them, and re-layouts: 90.3 us -> 12.3 us
  matrix products: 55.7 us -> 0 us
  Pallas kernels: 0 us -> 42.6 us
  blocking collectives: 39.6 us -> 0 us
  other arithmetic: 40.7 us -> 6.66 us
    dot_general x12 -> x0, matrix products: 55.7 us -> none  [the longest x4 36.6 us: spot_slopes(): jnp.dot(field.reshape(patterns * sub_count, 2 * flat), transform, precisi...]
    dynamic_slice x4 -> x0, local copies, waits for them, and re-layouts: 44.1 us -> none  [per_device(): slopes = lax.map(one_block, blocks).reshape(patterns, 2, sub_count)]
    pallas_call x0 -> x2, Pallas kernels: none -> 42.6 us  [the longest x1 30.3 us: per_device(): pl.pallas_call(functools.partial(gather_kernel, n), out_shape=jax.ShapeDt...]
    all_gather x1 -> x0, blocking collectives: 39.6 us -> none  [per_device(): lax.all_gather(shortened(slopes), 'tile', axis=2, tiled=True)]
    mul x7 -> x2, other arithmetic: 33.3 us -> 1.69 us  [the longest x1 1.17 us: per_device(): real, imag = (amp * jnp.cos(abe), amp * jnp.sin(abe))]
    reshape x8 -> x0, local copies, waits for them, and re-layouts: 28.3 us -> none  [the longest x4 18.8 us: spot_slopes(): phase_rows = phase_map.reshape(patterns, sub_count, flat)]
    add x5 -> x0, local copies, waits for them, and re-layouts: 10.6 us -> none  [the longest x1 5.57 us: per_device(): local_term.astype(jnp.float32) + from_lower.astype(jnp.float32)]
    add x3 -> x0, other arithmetic: 6.76 us -> none  [the longest x2 3.97 us: kron_tables(): jnp.kron(table_real, table_imag) + jnp.kron(table_imag, table_real)]
  transfers between devices with their start and end apart: 4 -> 4, of which waited for: 0 -> 0; matrix products, arithmetic and copies ran while one was open for 2% -> 16% of each run, Pallas kernels for 0% -> 0%
where the time goes in v1:
time: 73.7 us; the launch traced here: 73 us
  Pallas kernels  42.6 us (58%)
  local copies, waits for them, and re-layouts  12.3 us (17%)
  starting transfers between devices  11.3 us (15%)
  other arithmetic  6.66 us (9%)
    pallas_call x1, Pallas kernels, per_device(): pl.pallas_call(functools.partial(gather_kernel, n), out_shape=jax.ShapeDt...  30.3 us
    pallas_call x1, Pallas kernels, per_device(): pl.pallas_call(functools.partial(slopes_kernel, per_step, flat), grid=(su...  12.3 us
    ppermute x4, starting transfers between devices, passed_along(): lax.ppermute(value, axis, [(source, source + steps) for source in range(f...  11.3 us
    unnamed x25, local copies, waits for them, and re-layouts  4.05 us
    squeeze x1, local copies, waits for them, and re-layouts, per_device(): influence[0]  3.39 us
    mul x2, local copies, waits for them, and re-layouts, per_device(): real, imag = (amp * jnp.cos(abe), amp * jnp.sin(abe))  3.17 us
  transfers between devices with their start and end apart: 4, of which 0 were waited for; matrix products, arithmetic and copies ran while one was open for 16% of the time, Pallas kernels for 0%

profile of v1, /device:TPU:0, one launch (start us, length us, event | category | flops | bytes accessed | tf_op | source)
XLA Modules:
  0.0 73.0 jit_solution(541676475435677965)
XLA Ops:
  0.0 0.9 %copy.13 = s32[128,72]{1,0:T(8,128)S(1)} copy(s32[128,72]{0,1:T(8,128)} %param.7) | data formatting | bytes 73728 | tf_op args[0]
  0.9 0.0 copy-start.5
  0.9 1.3 %multiply_convert_fusion = bf16[128,72]{1,0:T(8,128)(2,1)} fusion(s32[128,72]{1,0:T(8,128)S(1)} %copy.13, f32[72]{0:T(128)} %param.8), kind=kLoop, calls=%fused_computation.6 | loop fusion | flops 27648 | bytes 55584 | tf_op jit(solution)/shard_map/convert_element_type | solution.py:152
  2.2 0.0 copy-start.10
  2.2 0.0 copy-start.7
  2.2 0.0 copy-start.8
  2.2 0.0 copy-start.9
  2.2 0.0 copy-start.11
  2.2 3.1 %collective-permute-start = (bf16[128,72]{1,0:T(8,128)(2,1)}, bf16[128,72]{1,0:T(8,128)(2,1)}, u32[]{:S(2)}, u32[]{:S(2)}) collective-permute-start(bf16[128,72]{1,0:T(8,128)(2,1)} %multiply_convert_fusion), channel_id=1, source_target_pairs={{0,1},{1,2},{2,3},{3,4},{4,5},{5,6},{6,7},{7,8},{8,9},{9,10},{10,1... | collective-permute-start | bytes 55304 | tf_op jit(solution)/shard_map/ppermute | solution.py:143
  5.3 0.0 copy-done.5
  5.3 1.3 %collective-permute-start.1 = (bf16[128,72]{1,0:T(8,128)(2,1)}, bf16[128,72]{1,0:T(8,128)(2,1)}, u32[]{:S(2)}, u32[]{:S(2)}) collective-permute-start(bf16[128,72]{1,0:T(8,128)(2,1)} %multiply_convert_fusion), channel_id=1, source_target_pairs={{1,0},{2,1},{3,2},{4,3},{5,4},{6,5},{7,6},{8,7},{9,8},{10,9},{11,1... | collective-permute-start | bytes 55304 | tf_op jit(solution)/shard_map/ppermute | solution.py:143
  6.6 0.0 copy-start.6
  6.6 0.0 copy-start
  6.6 3.4 %slice_bitcast_fusion = (bf16[72,8192]{1,0:T(8,128)(2,1)}, bf16[72,8192]{1,0:T(8,128)(2,1)}) fusion(bf16[3,72,8192]{2,1,0:T(8,128)(2,1)} %mid_ref.1), kind=kLoop, calls=%fused_computation | loop fusion | bytes 4718592 | tf_op jit(solution)/shard_map/squeeze | solution.py:153
  10.0 5.6 %collective-permute-start.2 = (bf16[72,8192]{1,0:T(8,128)(2,1)}, bf16[72,8192]{1,0:T(8,128)(2,1)}, u32[]{:S(2)}, u32[]{:S(2)}) collective-permute-start(bf16[72,8192]{1,0:T(8,128)(2,1)} %get-tuple-element.6), channel_id=1, source_target_pairs={{0,1},{1,2},{2,3},{3,4},{4,5},{5,6},{6,7},{7,8},{8,9},{9,10},{10,1... | collective-permute-start | bytes 3538952 | tf_op jit(solution)/shard_map/ppermute | solution.py:143
  15.6 1.3 %collective-permute-start.3 = (bf16[72,8192]{1,0:T(8,128)(2,1)}, bf16[72,8192]{1,0:T(8,128)(2,1)}, u32[]{:S(2)}, u32[]{:S(2)}) collective-permute-start(bf16[72,8192]{1,0:T(8,128)(2,1)} %get-tuple-element.5), channel_id=1, source_target_pairs={{1,0},{2,1},{3,2},{4,3},{5,4},{6,5},{7,6},{8,7},{9,8},{10,9},{11,1... | collective-permute-start | bytes 3538952 | tf_op jit(solution)/shard_map/ppermute | solution.py:143
  16.9 0.0 copy-done.10
  16.9 0.5 broadcast_multiply_fusion
  17.5 0.0 copy-done.7
  17.5 0.6 convert_bitcast_fusion.had_ref
  18.1 0.0 copy-done.6
  18.1 0.6 fusion
  18.7 0.0 copy-done.8
  18.7 0.0 copy-done.9
  18.7 1.2 %sine_multiply_fusion = (f32[32,16,16]{0,2,1:T(8,128)}, f32[32,16,16]{0,2,1:T(8,128)}) fusion(f32[32,16,16]{0,2,1:T(8,128)S(1)} %copy-done.8, f32[32,16,16]{0,2,1:T(8,128)S(1)} %copy-done.9), kind=kLoop, calls=%fused_computation.3 | loop fusion | flops 16384 | bytes 131072 | tf_op jit(solution)/shard_map/mul | solution.py:157
  19.9 0.0 copy-done.11
  19.9 0.6 convert_bitcast_fusion.1
  20.5 1.6 %copy.14.real_ref = f32[32,256]{1,0:T(8,128)} copy(f32[32,256]{0,1:T(8,128)} %bitcast.17) | data formatting | bytes 65536 | tf_op jit(solution)/shard_map/mul | solution.py:157
  22.0 1.6 %copy.15.imag_ref = f32[32,256]{1,0:T(8,128)} copy(f32[32,256]{0,1:T(8,128)} %bitcast.16) | data formatting | bytes 65536 | tf_op jit(solution)/shard_map/mul | solution.py:157
  23.6 0.8 %copy.16.mask_ref = f32[32,1]{1,0:T(8,128)S(1)} copy(f32[32,1]{0,1:T(1,128)} %convert_bitcast_fusion.1) | data formatting | bytes 256 | tf_op jit(solution)/shard_map/broadcast_in_dim | solution.py:158
  24.4 0.0 collective-permute-done
  24.4 0.0 collective-permute-done.1
  24.4 0.8 %pad_maximum_fusion.cmd_ref = bf16[3,128,72]{2,1,0:T(8,128)(2,1)S(1)} fusion(bf16[1,128,72]{2,1,0:T(8,128)(2,1)} %bitcast.2, bf16[1,128,72]{2,1,0:T(8,128)(2,1)} %fusion, bf16[1,128,72]{2,1,0:T(8,128)(2,1)} %bitcast), kind=kLoop, calls=%fused_computation.5 | loop fusion | flops 55296 | bytes 110592 | tf_op jit(solution)/shard_map/stack | solution.py:155
  25.2 0.0 collective-permute-done.2.low_ref
  25.2 0.0 collective-permute-done.3.up_ref
  25.2 0.0 copy-done
  25.2 0.0 copy-start.1
  25.2 1.0 %copy-done.1 = bf16[512,512]{1,0:T(8,128)(2,1)S(1)} copy-done((bf16[512,512]{1,0:T(8,128)(2,1)S(1)}, bf16[512,512]{1,0:T(8,128)(2,1)}, u32[]{:S(2)}) %copy-start.1) | copy-done | bytes 524312
  26.3 0.0 copy-start.2
  26.3 0.8 %copy-done.2 = f32[32,256]{1,0:T(8,128)S(1)} copy-done((f32[32,256]{1,0:T(8,128)S(1)}, f32[32,256]{1,0:T(8,128)}, u32[]{:S(2)}) %copy-start.2) | copy-done | bytes 32792
  27.0 0.0 copy-start.3
  27.0 0.8 %copy-done.3 = f32[32,256]{1,0:T(8,128)S(1)} copy-done((f32[32,256]{1,0:T(8,128)S(1)}, f32[32,256]{1,0:T(8,128)}, u32[]{:S(2)}) %copy-start.3) | copy-done | bytes 32792
  27.8 12.3 %slopes.1.mine_ref = bf16[2,32,128]{2,1,0:T(8,128)(2,1)S(1)} custom-call(bf16[3,128,72]{2,1,0:T(8,128)(2,1)S(1)} %pad_maximum_fusion.cmd_ref, bf16[3,72,8192]{2,1,0:T(8,128)(2,1)S(1)} %copy-done, bf16[72,8192]{1,0:T(8,128)(2,1)} %collective-permute-done.2.low_ref, bf16[72,8192]{1,0:T(8,128)(2,1)} %collective-permute-done.3.up_ref, f32[32,256]{1,0:T(8,128)S(1)} %copy-done.2, ...), custom_call_target="tpu_custom_call" | custom-call | tf_op jit(solution)/shard_map/slopes/pallas_call | solution.py:161
  40.1 0.0 copy-start.4
  40.1 0.6 copy-done.4
  40.7 30.3 %gather.1 = f32[2,72,512]{2,1,0:T(8,128)} custom-call(bf16[2,32,128]{2,1,0:T(8,128)(2,1)} %copy-done.4, bf16[72,128]{1,0:T(8,128)(2,1)} %convert_bitcast_fusion.had_ref), custom_call_target="tpu_custom_call" | custom-call | tf_op jit(solution)/shard_map/gather/pallas_call | solution.py:180
  71.0 1.1 %divide_bitcast_fusion = f32[72,2,512]{2,0,1:T(8,128)S(1)} fusion(f32[2,72,512]{2,1,0:T(8,128)} %gather.1, f32[72]{0:T(128)} %broadcast_multiply_fusion), kind=kLoop, calls=%fused_computation.2 | loop fusion | flops 73728 | bytes 590112 | tf_op jit(solution)/shard_map/div | solution.py:194
  72.1 0.9 %copy.17 = f32[72,2,512]{2,1,0:T(2,128)} copy(f32[72,2,512]{2,0,1:T(8,128)S(1)} %divide_bitcast_fusion) | data formatting | bytes 589824 | tf_op jit(solution)/shard_map/div | solution.py:194
Async XLA Ops:
  0.9 4.5 %copy-start.5 = (s32[128,72]{1,0:T(8,128)}, s32[128,72]{1,0:T(8,128)S(1)}, u32[]{:S(2)}) copy-start(s32[128,72]{1,0:T(8,128)S(1)} %copy.13) | copy-start | bytes 110596
  2.2 14.8 %copy-start.10 = (f32[72]{0:T(128)S(1)}, f32[72]{0:T(128)}, u32[]{:S(2)}) copy-start(f32[72]{0:T(128)} %param.8) | copy-start | bytes 868
  2.2 15.3 %copy-start.7 = (s32[128,72]{0,1:T(8,128)S(1)}, s32[128,72]{0,1:T(8,128)}, u32[]{:S(2)}) copy-start(s32[128,72]{0,1:T(8,128)} %param.7) | copy-start | bytes 110596
  2.2 16.5 %copy-start.8 = (f32[32,16,16]{0,2,1:T(8,128)S(1)}, f32[32,16,16]{0,2,1:T(8,128)}, u32[]{:S(2)}) copy-start(f32[32,16,16]{0,2,1:T(8,128)} %param.10) | copy-start | bytes 98308
  2.2 16.5 %copy-start.9 = (f32[32,16,16]{0,2,1:T(8,128)S(1)}, f32[32,16,16]{0,2,1:T(8,128)}, u32[]{:S(2)}) copy-start(f32[32,16,16]{0,2,1:T(8,128)} %param.11) | copy-start | bytes 98308
  2.2 17.7 %copy-start.11 = (s32[32]{0:T(128)S(1)}, s32[32]{0:T(128)}, u32[]{:S(2)}) copy-start(s32[32]{0:T(128)} %param.12) | copy-start | bytes 388
  2.2 22.2 %collective-permute-start = (bf16[128,72]{1,0:T(8,128)(2,1)}, bf16[128,72]{1,0:T(8,128)(2,1)}, u32[]{:S(2)}, u32[]{:S(2)}) collective-permute-start(bf16[128,72]{1,0:T(8,128)(2,1)} %multiply_convert_fusion), channel_id=1, source_target_pairs={{0,1},{1,2},{2,3},{3,4},{4,5},{5,6},{6,7},{7,8},{8,9},{9,10},{10,1... | collective-permute-start | bytes 55304 | tf_op jit(solution)/shard_map/ppermute | solution.py:143
  5.3 19.1 %collective-permute-start.1 = (bf16[128,72]{1,0:T(8,128)(2,1)}, bf16[128,72]{1,0:T(8,128)(2,1)}, u32[]{:S(2)}, u32[]{:S(2)}) collective-permute-start(bf16[128,72]{1,0:T(8,128)(2,1)} %multiply_convert_fusion), channel_id=1, source_target_pairs={{1,0},{2,1},{3,2},{4,3},{5,4},{6,5},{7,6},{8,7},{9,8},{10,9},{11,1... | collective-permute-start | bytes 55304 | tf_op jit(solution)/shard_map/ppermute | solution.py:143
  6.6 11.5 %copy-start.6 = (s32[128,72]{1,0:T(8,128)S(1)}, s32[128,72]{1,0:T(8,128)}, u32[]{:S(2)}) copy-start(s32[128,72]{1,0:T(8,128)} %copy-done.5) | copy-start | bytes 110596
  6.6 18.6 %copy-start = (bf16[3,72,8192]{2,1,0:T(8,128)(2,1)S(1)}, bf16[3,72,8192]{2,1,0:T(8,128)(2,1)}, u32[]{:S(2)}) copy-start(bf16[3,72,8192]{2,1,0:T(8,128)(2,1)} %mid_ref.1) | copy-start | bytes 10616836
  10.0 15.2 %collective-permute-start.2 = (bf16[72,8192]{1,0:T(8,128)(2,1)}, bf16[72,8192]{1,0:T(8,128)(2,1)}, u32[]{:S(2)}, u32[]{:S(2)}) collective-permute-start(bf16[72,8192]{1,0:T(8,128)(2,1)} %get-tuple-element.6), channel_id=1, source_target_pairs={{0,1},{1,2},{2,3},{3,4},{4,5},{5,6},{6,7},{7,8},{8,9},{9,10},{10,1... | collective-permute-start | bytes 3538952 | tf_op jit(solution)/shard_map/ppermute | solution.py:143
  15.6 9.6 %collective-permute-start.3 = (bf16[72,8192]{1,0:T(8,128)(2,1)}, bf16[72,8192]{1,0:T(8,128)(2,1)}, u32[]{:S(2)}, u32[]{:S(2)}) collective-permute-start(bf16[72,8192]{1,0:T(8,128)(2,1)} %get-tuple-element.5), channel_id=1, source_target_pairs={{1,0},{2,1},{3,2},{4,3},{5,4},{6,5},{7,6},{8,7},{9,8},{10,9},{11,1... | collective-permute-start | bytes 3538952 | tf_op jit(solution)/shard_map/ppermute | solution.py:143
  25.2 1.0 %copy-start.1 = (bf16[512,512]{1,0:T(8,128)(2,1)S(1)}, bf16[512,512]{1,0:T(8,128)(2,1)}, u32[]{:S(2)}) copy-start(bf16[512,512]{1,0:T(8,128)(2,1)} %constant.4.clone.table_ref) | copy-start | bytes 1572868
  26.3 0.8 %copy-start.2 = (f32[32,256]{1,0:T(8,128)S(1)}, f32[32,256]{1,0:T(8,128)}, u32[]{:S(2)}) copy-start(f32[32,256]{1,0:T(8,128)} %copy.14.real_ref) | copy-start | bytes 98308
  27.0 0.8 %copy-start.3 = (f32[32,256]{1,0:T(8,128)S(1)}, f32[32,256]{1,0:T(8,128)}, u32[]{:S(2)}) copy-start(f32[32,256]{1,0:T(8,128)} %copy.15.imag_ref) | copy-start | bytes 98308
  40.1 0.6 copy-start.4

commit v2 on v1

--- a/solution.py
+++ b/solution.py
@@ -84,22 +84,176 @@
     return (qu * p0 - pu * q0) * scale, (qv * p0 - pv * q0) * scale
 
 
-def slopes_kernel(per_step, flat, cmd_ref, mid_ref, low_ref, up_ref, real_ref, imag_ref, mask_ref, table_ref, out_ref):
-    rows_u, rows_v = [], []
-    for k in range(per_step):
-        cols = pl.ds(k * flat, flat)
-        phase = jnp.dot(cmd_ref[0], low_ref[:, cols], preferred_element_type=jnp.float32)
-        phase += jnp.dot(cmd_ref[1], mid_ref[0, :, cols], preferred_element_type=jnp.float32)
-        phase += jnp.dot(cmd_ref[2], up_ref[:, cols], preferred_element_type=jnp.float32)
-        along_u, along_v = spot_rows(phase, real_ref[k:k + 1, :], imag_ref[k:k + 1, :], table_ref[...])
-        rows_u.append(along_u)
-        rows_v.append(along_v)
-    mask = mask_ref[...]
-    out_ref[0] = (jnp.concatenate(rows_u, axis=0) * mask).astype(out_ref.dtype)
-    out_ref[1] = (jnp.concatenate(rows_v, axis=0) * mask).astype(out_ref.dtype)
-
-
-def gather_kernel(n, mine_ref, had_ref, out_ref, held, own_sem, send_sems, recv_sems):
+def diagonal_column(row):
+    k = row.shape[1]
+    shape = (k, k)
+    same = lax.broadcasted_iota(jnp.int32, shape, 0) == lax.broadcasted_iota(jnp.int32, shape, 1)
+    return jnp.sum(jnp.where(same, jnp.broadcast_to(row, shape), 0.0), axis=1, keepdims=True)
+
+
+def commands_of(had, stroke):
+    return (stroke * had.astype(jnp.float32).T).astype(jnp.bfloat16)
+
+
+def slopes_kernel(
+    n, chunks, per, flat,
+    had_ref, stroke_ref, infl_ref, amp_ref, abe_ref, mask_ref, table_ref,
+    out_ref,
+    mid_buf, low_buf, up_buf, had_low, had_up, stroke_low, stroke_up, real, imag, rows,
+    mid_sems, send_sems, recv_sems, cmd_send, cmd_recv,
+):
+    me = lax.axis_index("tile")
+    has_low, has_up = me > 0, me < n - 1
+    low_id, up_id = {"tile": jnp.maximum(me - 1, 0)}, {"tile": jnp.minimum(me + 1, n - 1)}
+    width = per * flat
+    barrier = pltpu.get_barrier_semaphore()
+
+    @pl.when(has_low)
+    def _():
+        pl.semaphore_signal(barrier, inc=1, device_id=low_id, device_id_type=MESH)
+
+    @pl.when(has_up)
+    def _():
+        pl.semaphore_signal(barrier, inc=1, device_id=up_id, device_id_type=MESH)
+
+    def columns(c):
+        return pl.ds(pl.multiple_of(c * width, width), width)
+
+    def mid_copy(c):
+        return pltpu.make_async_copy(infl_ref.at[1, :, columns(c)], mid_buf.at[c], mid_sems.at[c])
+
+    def remote(src, dst, send, recv, device):
+        return pltpu.make_async_remote_copy(
+            src_ref=src, dst_ref=dst, send_sem=send, recv_sem=recv, device_id=device, device_id_type=MESH
+        )
+
+    def to_up(c):
+        return remote(infl_ref.at[2, :, columns(c)], low_buf.at[c], send_sems.at[0, c], recv_sems.at[0, c], up_id)
+
+    def to_low(c):
+        return remote(infl_ref.at[0, :, columns(c)], up_buf.at[c], send_sems.at[1, c], recv_sems.at[1, c], low_id)
+
+    def cmds_up():
+        return (
+            remote(had_ref, had_low, cmd_send.at[0], cmd_recv.at[0], up_id),
+            remote(stroke_ref, stroke_low, cmd_send.at[1], cmd_recv.at[1], up_id),
+        )
+
+    def cmds_low():
+        return (
+            remote(had_ref, had_up, cmd_send.at[2], cmd_recv.at[2], low_id),
+            remote(stroke_ref, stroke_up, cmd_send.at[3], cmd_recv.at[3], low_id),
+        )
+
+    inner = jnp.logical_and(has_low, has_up)
+
+    @pl.when(inner)
+    def _():
+        pl.semaphore_wait(barrier, 2)
+
+    @pl.when(jnp.logical_not(inner))
+    def _():
+        pl.semaphore_wait(barrier, 1)
+
+    @pl.when(has_up)
+    def _():
+        for copy in cmds_up():
+            copy.start()
+
+    @pl.when(has_low)
+    def _():
+        for copy in cmds_low():
+            copy.start()
+
+    @pl.loop(0, chunks)
+    def _(c):
+        @pl.when(has_up)
+        def _():
+            to_up(c).start()
+
+        @pl.when(has_low)
+        def _():
+            to_low(c).start()
+
+        mid_copy(c).start()
+
+    @pl.when(jnp.logical_not(has_low))
+    def _():
+        had_low[...] = jnp.zeros_like(had_low)
+        stroke_low[...] = jnp.zeros_like(stroke_low)
+        low_buf[...] = jnp.zeros_like(low_buf)
+
+    @pl.when(jnp.logical_not(has_up))
+    def _():
+        had_up[...] = jnp.zeros_like(had_up)
+        stroke_up[...] = jnp.zeros_like(stroke_up)
+        up_buf[...] = jnp.zeros_like(up_buf)
+
+    cs, sn = cos_sin(abe_ref[...])
+    whole_real, whole_imag = (amp_ref[...] * cs).T, (amp_ref[...] * sn).T
+    for c in range(chunks):
+        real[c] = whole_real[c * per:(c + 1) * per]
+        imag[c] = whole_imag[c * per:(c + 1) * per]
+
+    @pl.when(has_up)
+    def _():
+        for copy in cmds_up():
+            copy.wait_send()
+        for copy in cmds_low():
+            copy.wait_recv()
+
+    @pl.when(has_low)
+    def _():
+        for copy in cmds_low():
+            copy.wait_send()
+        for copy in cmds_up():
+            copy.wait_recv()
+
+    mid_cmds = commands_of(had_ref[...], stroke_ref[...])
+    low_cmds = commands_of(had_low[...], stroke_low[...])
+    up_cmds = commands_of(had_up[...], stroke_up[...])
+
+    @pl.loop(0, chunks)
+    def _(c):
+        mid_copy(c).wait()
+
+        @pl.when(has_low)
+        def _():
+            to_up(c).wait_recv()
+
+        @pl.when(has_up)
+        def _():
+            to_low(c).wait_recv()
+
+        rows_u, rows_v = [], []
+        for k in range(per):
+            cols = slice(k * flat, (k + 1) * flat)
+            phase = jnp.dot(low_cmds, low_buf[c, :, cols], preferred_element_type=jnp.float32)
+            phase += jnp.dot(mid_cmds, mid_buf[c, :, cols], preferred_element_type=jnp.float32)
+            phase += jnp.dot(up_cmds, up_buf[c, :, cols], preferred_element_type=jnp.float32)
+            along_u, along_v = spot_rows(phase, real[c, k:k + 1, :], imag[c, k:k + 1, :], table_ref[...])
+            rows_u.append(along_u)
+            rows_v.append(along_v)
+        rows[c, 0] = jnp.concatenate(rows_u, axis=0)
+        rows[c, 1] = jnp.concatenate(rows_v, axis=0)
+
+    mask = diagonal_column(mask_ref[...].astype(jnp.float32))
+    for j in range(2):
+        whole = jnp.concatenate([rows[c, j] for c in range(chunks)], axis=0)
+        out_ref[j] = (whole * mask).astype(out_ref.dtype)
+
+    @pl.loop(0, chunks)
+    def _(c):
+        @pl.when(has_up)
+        def _():
+            to_up(c).wait_send()
+
+        @pl.when(has_low)
+        def _():
+            to_low(c).wait_send()
+
+
+def gather_kernel(n, mine_ref, had_ref, stroke_ref, out_ref, held, own_sem, send_sems, recv_sems):
     me = lax.axis_index("tile")
     subs = mine_ref.shape[1]
     barrier = pltpu.get_barrier_semaphore()
@@ -127,6 +281,9 @@
     def _(k):
         push(k).start()
 
+    patterns = had_ref.shape[1]
+    signs = had_ref[...].astype(jnp.float32).astype(jnp.bfloat16)
+    scale = patterns * diagonal_column(stroke_ref[...])
     own.wait()
 
     @pl.loop(1, n)
@@ -134,13 +291,8 @@
         push(k).wait()
 
     for c in range(2):
-        out_ref[c] = lax.dot_general(had_ref[...], held[c], NT, preferred_element_type=jnp.float32)
-
-
-def passed_along(value, axis, steps):
-    count = lax.axis_size(axis)
-    first, last = (max(0, -steps), min(count, count - steps))
-    return lax.ppermute(value, axis, [(source, source + steps) for source in range(first, last)])
+        summed = lax.dot_general(signs, held[c], NT, preferred_element_type=jnp.float32)
+        out_ref[:, c, :] = summed / scale
 
 
 def per_device(hadamard, stroke, influence, amplitude, aberration, valid_mask):
@@ -148,40 +300,46 @@
     patterns, acts = hadamard.shape
     subs, samples = amplitude.shape[0], amplitude.shape[1]
     flat = samples * samples
-    per_step = math.gcd(subs, 16)
-    commands = (stroke[None, :] * hadamard.astype(jnp.float32)).astype(jnp.bfloat16)
-    low_slab, up_slab = passed_along(influence[2], "tile", 1), passed_along(influence[0], "tile", -1)
-    low_cmds, up_cmds = passed_along(commands, "tile", 1), passed_along(commands, "tile", -1)
-    cmds = jnp.stack([low_cmds, commands, up_cmds])
-    amp, abe = amplitude.reshape(subs, flat), aberration.reshape(subs, flat)
-    real, imag = amp * jnp.cos(abe), amp * jnp.sin(abe)
-    mask = valid_mask.astype(jnp.float32)[:, None]
+    per = math.gcd(subs, 4)
+    chunks = subs // per
+    had = hadamard.T
+    amp = amplitude.transpose(1, 2, 0).reshape(flat, subs)
+    abe = aberration.transpose(1, 2, 0).reshape(flat, subs)
+    stroke = stroke.reshape(1, acts)
+    mask = valid_mask.reshape(1, subs)
     table = jnp.asarray(dft_table(samples, PIX), dtype=jnp.bfloat16)
-    width = per_step * flat
+    vmem = pl.BlockSpec(memory_space=pltpu.VMEM)
+    slab = pltpu.VMEM((chunks, acts, per * flat), jnp.bfloat16)
     slopes = pl.pallas_call(
-        functools.partial(slopes_kernel, per_step, flat),
-        grid=(subs // per_step,),
+        functools.partial(slopes_kernel, n, chunks, per, flat),
         out_shape=jax.ShapeDtypeStruct((2, subs, patterns), jnp.bfloat16),
-        in_specs=[
-            pl.BlockSpec((3, patterns, acts), lambda i: (0, 0, 0)),
-            pl.BlockSpec((1, acts, width), lambda i: (1, 0, i)),
-            pl.BlockSpec((acts, width), lambda i: (0, i)),
-            pl.BlockSpec((acts, width), lambda i: (0, i)),
-            pl.BlockSpec((per_step, flat), lambda i: (i, 0)),
-            pl.BlockSpec((per_step, flat), lambda i: (i, 0)),
-            pl.BlockSpec((per_step, 1), lambda i: (i, 0)),
-            pl.BlockSpec((2 * flat, 2 * flat), lambda i: (0, 0)),
+        in_specs=[vmem, vmem, pl.BlockSpec(memory_space=pltpu.HBM), vmem, vmem, vmem, vmem],
+        out_specs=vmem,
+        scratch_shapes=[
+            slab, slab, slab,
+            pltpu.VMEM((acts, patterns), jnp.int32),
+            pltpu.VMEM((acts, patterns), jnp.int32),
+            pltpu.VMEM((1, acts), jnp.float32),
+            pltpu.VMEM((1, acts), jnp.float32),
+            pltpu.VMEM((chunks, per, flat), jnp.float32),
+            pltpu.VMEM((chunks, per, flat), jnp.float32),
+            pltpu.VMEM((chunks, 2, per, patterns), jnp.float32),
+            pltpu.SemaphoreType.DMA((chunks,)),
+            pltpu.SemaphoreType.DMA((2, chunks)),
+            pltpu.SemaphoreType.DMA((2, chunks)),
+            pltpu.SemaphoreType.DMA((4,)),
+            pltpu.SemaphoreType.DMA((4,)),
         ],
-        out_specs=pl.BlockSpec((2, per_step, patterns), lambda i: (0, i, 0)),
-        compiler_params=pltpu.CompilerParams(vmem_limit_bytes=40 * 1024 * 1024),
+        compiler_params=pltpu.CompilerParams(
+            collective_id=1, has_side_effects=True, vmem_limit_bytes=40 * 1024 * 1024
+        ),
         name="slopes",
-    )(cmds, influence, low_slab, up_slab, real, imag, mask, table)
-    signs = hadamard.T.astype(jnp.bfloat16)
-    summed = pl.pallas_call(
+    )(had, stroke, influence, amp, abe, mask, table)
+    return pl.pallas_call(
         functools.partial(gather_kernel, n),
-        out_shape=jax.ShapeDtypeStruct((2, acts, n * subs), jnp.float32),
-        in_specs=[pl.BlockSpec(memory_space=pltpu.VMEM)] * 2,
-        out_specs=pl.BlockSpec(memory_space=pltpu.VMEM),
+        out_shape=jax.ShapeDtypeStruct((acts, 2, n * subs), jnp.float32),
+        in_specs=[vmem] * 3,
+        out_specs=vmem,
         scratch_shapes=[
             pltpu.VMEM((2, n * subs, patterns), jnp.bfloat16),
             pltpu.SemaphoreType.DMA,
@@ -190,8 +348,7 @@
         ],
         compiler_params=pltpu.CompilerParams(collective_id=0, has_side_effects=True),
         name="gather",
-    )(slopes, signs)
-    return summed.transpose(1, 0, 2) / (patterns * stroke)[:, None, None]
+    )(slopes, had, stroke)
 
 
 def solution(mesh):

time: 73.7 us -> 53.4 us (0.72)
  starting transfers between devices: 11.3 us -> 0 us
  other arithmetic: 6.66 us -> 0 us
  local copies, waits for them, and re-layouts: 12.3 us -> 9.22 us
  Pallas kernels: 42.6 us -> 43.8 us
    ppermute x4 -> x0, starting transfers between devices: 11.3 us -> none  [passed_along(): lax.ppermute(value, axis, [(source, source + steps) for source in range(f...]
    unnamed x25 -> x17, local copies, waits for them, and re-layouts: 4.05 us -> 9.22 us
    pallas_call x1, Pallas kernels: 12.3 us -> 17.2 us  [per_device(): pl.pallas_call(functools.partial(slopes_kernel, n, chunks, per, flat), ou...]
    pallas_call x1, Pallas kernels: 30.3 us -> 26.6 us  [per_device(): pl.pallas_call(functools.partial(gather_kernel, n), out_shape=jax.ShapeDt...]
    squeeze x1 -> x0, local copies, waits for them, and re-layouts: 3.39 us -> none  [per_device(): influence[0]]
    mul x2 -> x0, local copies, waits for them, and re-layouts: 3.17 us -> none  [per_device(): real, imag = (amp * jnp.cos(abe), amp * jnp.sin(abe))]
    convert_element_type x2 -> x0, other arithmetic: 1.89 us -> none  [the longest x1 1.29 us: per_device(): (stroke[None, :] * hadamard.astype(jnp.float32)).astype(jnp.bfloat16)]
    mul x2 -> x0, other arithmetic: 1.69 us -> none  [the longest x1 1.17 us: per_device(): real, imag = (amp * jnp.cos(abe), amp * jnp.sin(abe))]
  transfers between devices with their start and end apart: 4 -> 0, of which waited for: 0 -> 0; matrix products, arithmetic and copies ran while one was open for 16% -> 0% of each run, Pallas kernels for 0% -> 0%
where the time goes in v2:
time: 53.4 us; the launch traced here: 53 us
  Pallas kernels  43.8 us (82%)
  local copies, waits for them, and re-layouts  9.22 us (17%)
    pallas_call x1, Pallas kernels, per_device(): pl.pallas_call(functools.partial(gather_kernel, n), out_shape=jax.ShapeDt...  26.6 us
    pallas_call x1, Pallas kernels, per_device(): pl.pallas_call(functools.partial(slopes_kernel, n, chunks, per, flat), ou...  17.2 us
    unnamed x17, local copies, waits for them, and re-layouts  9.22 us

profile of v2, /device:TPU:0, one launch (start us, length us, event | category | flops | bytes accessed | tf_op | source)
XLA Modules:
  0.0 53.0 jit_solution(14319126017734123154)
XLA Ops:
  0.0 0.0 copy-start
  0.0 2.0 %copy-done = bf16[3,72,8192]{2,1,0:T(8,128)(2,1)S(1)} copy-done((bf16[3,72,8192]{2,1,0:T(8,128)(2,1)S(1)}, bf16[3,72,8192]{2,1,0:T(8,128)(2,1)}, u32[]{:S(2)}) %copy-start) | copy-done | bytes 3538968
  2.0 0.0 copy-start.1
  2.0 1.0 %copy-done.1 = bf16[512,512]{1,0:T(8,128)(2,1)S(1)} copy-done((bf16[512,512]{1,0:T(8,128)(2,1)S(1)}, bf16[512,512]{1,0:T(8,128)(2,1)}, u32[]{:S(2)}) %copy-start.1) | copy-done | bytes 524312
  3.0 0.0 copy-start.2
  3.0 0.8 %copy-done.2 = s32[128,72]{0,1:T(8,128)S(1)} copy-done((s32[128,72]{0,1:T(8,128)S(1)}, s32[128,72]{0,1:T(8,128)}, u32[]{:S(2)}) %copy-start.2) | copy-done | bytes 36888
  3.8 0.0 copy-start.3
  3.8 0.9 %copy-done.3 = f32[32,16,16]{0,2,1:T(8,128)S(1)} copy-done((f32[32,16,16]{0,2,1:T(8,128)S(1)}, f32[32,16,16]{0,2,1:T(8,128)}, u32[]{:S(2)}) %copy-start.3) | copy-done | bytes 32792
  4.7 0.0 copy-start.4
  4.7 0.9 %copy-done.4 = f32[32,16,16]{0,2,1:T(8,128)S(1)} copy-done((f32[32,16,16]{0,2,1:T(8,128)S(1)}, f32[32,16,16]{0,2,1:T(8,128)}, u32[]{:S(2)}) %copy-start.4) | copy-done | bytes 32792
  5.6 0.0 copy-start.6
  5.6 0.7 %copy-done.6 = f32[72]{0:T(128)S(1)} copy-done((f32[72]{0:T(128)S(1)}, f32[72]{0:T(128)}, u32[]{:S(2)}) %copy-start.6) | copy-done | bytes 312
  6.3 0.0 copy-start.7
  6.3 0.7 %copy-done.7 = s32[32]{0:T(128)S(1)} copy-done((s32[32]{0:T(128)S(1)}, s32[32]{0:T(128)}, u32[]{:S(2)}) %copy-start.7) | copy-done | bytes 152
  6.9 17.2 %slopes.1.mine_ref = bf16[2,32,128]{2,1,0:T(8,128)(2,1)S(1)} custom-call(s32[72,128]{1,0:T(8,128)S(1)} %bitcast.10, f32[1,72]{1,0:T(1,128)S(1)} %bitcast.14, bf16[3,72,8192]{2,1,0:T(8,128)(2,1)S(1)} %copy-done, f32[256,32]{1,0:T(8,128)S(1)} %bitcast.11, f32[256,32]{1,0:T(8,128)S(1)} %bitcast.12, s32[1,32]{1,0:T(1,128)S(1)} %bitcast.15, ...), custom_call_target="tpu_custom_call" | custom-call | tf_op jit(solution)/shard_map/slopes/pallas_call | solution.py:313
  24.1 0.0 copy-start.5
  24.1 0.6 %copy-done.5 = bf16[2,32,128]{2,1,0:T(8,128)(2,1)} copy-done((bf16[2,32,128]{2,1,0:T(8,128)(2,1)}, bf16[2,32,128]{2,1,0:T(8,128)(2,1)S(1)}, u32[]{:S(2)}) %copy-start.5) | copy-done | bytes 16408
  24.7 26.6 %gather.1 = f32[72,2,512]{2,1,0:T(2,128)} custom-call(bf16[2,32,128]{2,1,0:T(8,128)(2,1)} %copy-done.5, s32[72,128]{1,0:T(8,128)} %bitcast.9, f32[1,72]{1,0:T(1,128)} %bitcast.13), custom_call_target="tpu_custom_call" | custom-call | tf_op jit(solution)/shard_map/gather/pallas_call | solution.py:338
  51.3 1.7 %copy.9 = f32[72,2,512]{2,1,0:T(2,128)} copy(f32[72,2,512]{2,1,0:T(2,128)} %gather.1) | data formatting | bytes 589824
Async XLA Ops:
  0.0 2.0 %copy-start = (bf16[3,72,8192]{2,1,0:T(8,128)(2,1)S(1)}, bf16[3,72,8192]{2,1,0:T(8,128)(2,1)}, u32[]{:S(2)}) copy-start(bf16[3,72,8192]{2,1,0:T(8,128)(2,1)} %infl_ref.1) | copy-start | bytes 10616836
  2.0 1.0 %copy-start.1 = (bf16[512,512]{1,0:T(8,128)(2,1)S(1)}, bf16[512,512]{1,0:T(8,128)(2,1)}, u32[]{:S(2)}) copy-start(bf16[512,512]{1,0:T(8,128)(2,1)} %constant.2.clone.table_ref) | copy-start | bytes 1572868
  3.0 0.8 %copy-start.2 = (s32[128,72]{0,1:T(8,128)S(1)}, s32[128,72]{0,1:T(8,128)}, u32[]{:S(2)}) copy-start(s32[128,72]{0,1:T(8,128)} %param.7) | copy-start | bytes 110596
  3.8 0.9 %copy-start.3 = (f32[32,16,16]{0,2,1:T(8,128)S(1)}, f32[32,16,16]{0,2,1:T(8,128)}, u32[]{:S(2)}) copy-start(f32[32,16,16]{0,2,1:T(8,128)} %param.10) | copy-start | bytes 98308
  4.7 0.9 %copy-start.4 = (f32[32,16,16]{0,2,1:T(8,128)S(1)}, f32[32,16,16]{0,2,1:T(8,128)}, u32[]{:S(2)}) copy-start(f32[32,16,16]{0,2,1:T(8,128)} %param.11) | copy-start | bytes 98308
  5.6 0.7 %copy-start.6 = (f32[72]{0:T(128)S(1)}, f32[72]{0:T(128)}, u32[]{:S(2)}) copy-start(f32[72]{0:T(128)} %param.8) | copy-start | bytes 868
  6.3 0.7 %copy-start.7 = (s32[32]{0:T(128)S(1)}, s32[32]{0:T(128)}, u32[]{:S(2)}) copy-start(s32[32]{0:T(128)} %param.12) | copy-start | bytes 388
  24.1 0.6 %copy-start.5 = (bf16[2,32,128]{2,1,0:T(8,128)(2,1)}, bf16[2,32,128]{2,1,0:T(8,128)(2,1)S(1)}, u32[]{:S(2)}) copy-start(bf16[2,32,128]{2,1,0:T(8,128)(2,1)S(1)} %slopes.1.mine_ref) | copy-start | bytes 49156
